TPU v7x, 32 devices: a whole 2x2x4 slice. The times are simulated.
32 devices in a mesh: dp: 8 (over z, x), head: 4 (over y, core).
Axes of the slice: x: 2, y: 2, z: 4, core: 2. Of those that a mesh axis runs over, the one named last changes fastest.
Arguments:
- tokens: bfloat16 [11840, 768], P(('dp', 'head')), may hold values from -6 to 6
- caption_len: int32 [64], P('dp'), may hold values from 5 to 40, as said below
- first_gain: bfloat16 [768], P(('dp', 'head')), may hold values from 0.5 to 1.5
- first_shift: bfloat16 [768], P(('dp', 'head')), may hold values from -3 to 3
- qkv_weight: bfloat16 [768, 3, 768], P('dp', None, 'head'), may hold values from -0.21875 to 0.21875
- qkv_bias: bfloat16 [2, 768], P(None, ('head', 'dp')), may hold values from -3 to 3
- out_weight: bfloat16 [768, 768], P(('dp', 'head')), may hold values from -1.25 to 1.25
- out_bias: bfloat16 [768], P(('dp', 'head')), may hold values from -3 to 3
- second_gain: bfloat16 [768], P(('dp', 'head')), may hold values from 0.5 to 1.5
- second_shift: bfloat16 [768], P(('dp', 'head')), may hold values from -3 to 3
- up_weight: bfloat16 [768, 3072], P('dp', 'head'), may hold values from -0.21875 to 0.21875
- up_bias: bfloat16 [3072], P(('head', 'dp')), may hold values from -3 to 3
- down_weight: bfloat16 [3072, 768], P('head', 'dp'), may hold values from -0.109375 to 0.109375
- down_bias: bfloat16 [768], P(('dp', 'head')), may hold values from -3 to 3
- output_grad: bfloat16 [11840, 768], P(('dp', 'head')), may hold values from -6 to 6
Outputs:
- layer_out: bfloat16 [11840, 768], P(('dp', 'head'))
- tokens_grad: bfloat16 [11840, 768], P(('dp', 'head'))
- first_gain_grad: float32 [768], P(('dp', 'head'))
- first_shift_grad: float32 [768], P(('dp', 'head'))
- qkv_weight_grad: float32 [768, 3, 768], P('dp', None, 'head')
- qkv_bias_grad: float32 [2, 768], P(None, ('head', 'dp'))
- out_weight_grad: float32 [768, 768], P(('dp', 'head'))
- out_bias_grad: float32 [768], P(('dp', 'head'))
- second_gain_grad: float32 [768], P(('dp', 'head'))
- second_shift_grad: float32 [768], P(('dp', 'head'))
- up_weight_grad: float32 [768, 3072], P('dp', 'head')
- up_bias_grad: float32 [3072], P(('head', 'dp'))
- down_weight_grad: float32 [3072, 768], P('head', 'dp')
- down_bias_grad: float32 [768], P(('dp', 'head'))
Inputs may be any that keep to these rules, and one draw needn't show every extreme that they name: Each pair's caption fills its first caption_len slots; some pair's caption fills all 40 slots.
All inputs are finite; a program needn't handle non-finite values.
Results may differ from a plain program's by a relative error of at most 0.014.
Values may be sent and summed in bfloat16 or wider, within the bound.
No kernel may reach another device: no remote copies, remote signals or barrier semaphores. Data moves between devices by JAX's collectives and lax.ppermute only.
A program may use at most 128 MiB of HBM per device.

v0:
```python
from functools import partial
import jax
import jax.numpy as jnp
from jax import lax
from jax.sharding import PartitionSpec as P

HEAD_DIM = 64
TEXT = 40


def norm_rows(values, gain, shift):
    centre = jnp.mean(values, axis=-1, keepdims=True)
    spread = values - centre
    second = jnp.mean(spread * spread, axis=-1, keepdims=True)
    return spread * lax.rsqrt(second + 1e-06) * gain + shift


def contract_rows(former, latter):
    return lax.dot_general(
        former, latter, (((0,), (0,)), ((), ())), preferred_element_type=jnp.float32
    )


def times_transposed(former, latter):
    return lax.dot_general(
        former, latter, (((1,), (1,)), ((), ())), preferred_element_type=jnp.float32
    )


def column_sum(matrix):
    return jnp.sum(matrix.astype(jnp.float32), axis=0)


def local(
    tokens,
    caption_len,
    first_gain,
    first_shift,
    qkv_weight,
    qkv_bias,
    out_weight,
    out_bias,
    second_gain,
    second_shift,
    up_weight,
    up_bias,
    down_weight,
    down_bias,
    output_grad,
):
    width = tokens.shape[1]
    gain_one, shift_one, w_out, b_out, gain_two, shift_two, b_down = (
        lax.all_gather(first_gain, ("dp", "head"), axis=0, tiled=True),
        lax.all_gather(first_shift, ("dp", "head"), axis=0, tiled=True),
        lax.all_gather(out_weight, ("dp", "head"), axis=0, tiled=True),
        lax.all_gather(out_bias, ("dp", "head"), axis=0, tiled=True),
        lax.all_gather(second_gain, ("dp", "head"), axis=0, tiled=True),
        lax.all_gather(second_shift, ("dp", "head"), axis=0, tiled=True),
        lax.all_gather(down_bias, ("dp", "head"), axis=0, tiled=True),
    )
    w_qkv, b_qkv, w_up, b_up, w_down = (
        lax.all_gather(qkv_weight, "dp", axis=0, tiled=True),
        lax.all_gather(qkv_bias, "dp", axis=1, tiled=True),
        lax.all_gather(up_weight, "dp", axis=0, tiled=True),
        lax.all_gather(up_bias, "dp", axis=0, tiled=True),
        lax.all_gather(down_weight, "dp", axis=1, tiled=True),
    )
    local_width = w_qkv.shape[2]
    heads_local = local_width // HEAD_DIM
    flat_qkv = w_qkv.reshape(width, 3 * local_width)
    tok_rows = tokens.astype(jnp.float32)
    normed, first_pull = jax.vjp(
        norm_rows, tok_rows, gain_one.astype(jnp.float32), shift_one.astype(jnp.float32)
    )
    normed_low = normed.astype(jnp.bfloat16)
    whole = lax.all_gather(normed_low, "head", axis=0, tiled=True)
    group_rows = whole.shape[0]
    item_count = caption_len.shape[0]
    seq_length = group_rows // item_count
    projected = jnp.dot(whole, flat_qkv, preferred_element_type=jnp.float32).reshape(
        group_rows, 3, local_width
    )
    bias_rows = jnp.stack([b_qkv[0], jnp.zeros_like(b_qkv[0]), b_qkv[1]]).astype(jnp.float32)
    packed = (
        (projected + bias_rows)
        .astype(jnp.bfloat16)
        .reshape(item_count, seq_length, 3, heads_local, HEAD_DIM)
    )
    queries = packed[:, :, 0]
    key_rows = packed[:, :, 1]
    value_rows = packed[:, :, 2]
    score_scale = HEAD_DIM ** (-0.5)
    position = jnp.arange(seq_length, dtype=jnp.int32)
    visible = ((position[None, :] >= TEXT) | (position[None, :] < caption_len[:, None]))[
        :, None, None, :
    ]

    def masked_scores():
        product = (
            jnp.einsum("ishd,ithd->ihst", queries, key_rows, preferred_element_type=jnp.float32)
            * score_scale
        )
        return jnp.where(visible, product, -1000000000.0)

    scores = masked_scores()
    highest_score = jnp.max(scores, axis=-1, keepdims=True)
    unnormed = jnp.exp(scores - highest_score)
    row_totals = jnp.sum(unnormed, axis=-1, keepdims=True)
    attn_probs = unnormed / row_totals
    log_total = highest_score + jnp.log(row_totals)
    probs_low = attn_probs.astype(jnp.bfloat16)
    context = jnp.einsum(
        "ihst,ithd->ishd", probs_low, value_rows, preferred_element_type=jnp.float32
    )
    context_low = context.astype(jnp.bfloat16).reshape(group_rows, local_width)
    ctx_rows = lax.all_to_all(context_low, "head", split_axis=0, concat_axis=1, tiled=True)
    middle = tok_rows + (
        jnp.dot(ctx_rows, w_out, preferred_element_type=jnp.float32) + b_out.astype(jnp.float32)
    )
    hidden_in, second_pull = jax.vjp(
        norm_rows, middle, gain_two.astype(jnp.float32), shift_two.astype(jnp.float32)
    )
    hidden_low = hidden_in.astype(jnp.bfloat16)
    hidden_group = lax.all_gather(hidden_low, "head", axis=0, tiled=True)
    up_proj = jnp.dot(hidden_group, w_up, preferred_element_type=jnp.float32) + b_up.astype(
        jnp.float32
    )
    active, gelu_pull = jax.vjp(partial(jax.nn.gelu, approximate=False), up_proj)
    active_low = active.astype(jnp.bfloat16)
    branch_part = jnp.dot(active_low, w_down, preferred_element_type=jnp.float32)
    branch = lax.psum_scatter(
        branch_part.astype(jnp.bfloat16), "head", scatter_dimension=0, tiled=True
    ).astype(jnp.float32)
    layer_out = (middle + (branch + b_down.astype(jnp.float32))).astype(jnp.bfloat16)
    w_out = lax.all_gather(out_weight, ("dp", "head"), axis=0, tiled=True)
    w_qkv, w_up, w_down = (
        lax.all_gather(qkv_weight, "dp", axis=0, tiled=True),
        lax.all_gather(up_weight, "dp", axis=0, tiled=True),
        lax.all_gather(down_weight, "dp", axis=1, tiled=True),
    )
    flat_qkv = w_qkv.reshape(width, 3 * local_width)
    grad_top = output_grad.astype(jnp.float32)
    grad_low = grad_top.astype(jnp.bfloat16)
    down_bias_part = column_sum(grad_low)
    grad_group = lax.all_gather(grad_low, "head", axis=0, tiled=True)
    down_weight_part = contract_rows(active_low, grad_group)
    (grad_up,) = gelu_pull(times_transposed(grad_group, w_down))
    up_low = grad_up.astype(jnp.bfloat16)
    up_bias_part = column_sum(up_low)
    up_weight_part = contract_rows(hidden_group, up_low)
    grad_hidden = lax.psum_scatter(
        times_transposed(up_low, w_up).astype(jnp.bfloat16), "head", scatter_dimension=0, tiled=True
    ).astype(jnp.float32)
    grad_middle_part, gain_two_part, shift_two_part = second_pull(grad_hidden)
    grad_middle = grad_top + grad_middle_part
    middle_low = grad_middle.astype(jnp.bfloat16)
    out_bias_part = column_sum(middle_low)
    out_weight_part = contract_rows(ctx_rows, middle_low)
    grad_ctx = times_transposed(middle_low, w_out).astype(jnp.bfloat16)
    grad_context = lax.all_to_all(
        grad_ctx, "head", split_axis=1, concat_axis=0, tiled=True
    ).reshape(item_count, seq_length, heads_local, HEAD_DIM)
    scores = masked_scores()
    attn_probs = jnp.exp(scores - log_total)
    probs_low = attn_probs.astype(jnp.bfloat16)
    grad_probs = jnp.einsum(
        "ishd,ithd->ihst", grad_context, value_rows, preferred_element_type=jnp.float32
    )
    value_grad = jnp.einsum(
        "ihst,ishd->ithd", probs_low, grad_context, preferred_element_type=jnp.float32
    ).astype(jnp.bfloat16)
    grad_scores = attn_probs * (
        grad_probs - jnp.sum(attn_probs * grad_probs, axis=-1, keepdims=True)
    )
    scores_low = grad_scores.astype(jnp.bfloat16)
    query_grad = (
        jnp.einsum("ihst,ithd->ishd", scores_low, key_rows, preferred_element_type=jnp.float32)
        * score_scale
    ).astype(jnp.bfloat16)
    key_grad = (
        jnp.einsum("ihst,ishd->ithd", scores_low, queries, preferred_element_type=jnp.float32)
        * score_scale
    ).astype(jnp.bfloat16)
    grad_packed = jnp.stack([query_grad, key_grad, value_grad], axis=2).reshape(
        group_rows, 3 * local_width
    )
    qkv_weight_part = contract_rows(whole, grad_packed).reshape(width, 3, local_width)
    qkv_bias_part = jnp.stack(
        [column_sum(grad_packed[:, :local_width]), column_sum(grad_packed[:, 2 * local_width :])]
    )
    own_grads = lax.all_to_all(
        grad_packed.reshape(group_rows, 3, local_width),
        "head",
        split_axis=0,
        concat_axis=2,
        tiled=True,
    )
    all_columns = lax.all_gather(w_qkv, "head", axis=2, tiled=True)
    grad_normed = times_transposed(
        own_grads.reshape(own_grads.shape[0], 3 * width), all_columns.reshape(width, 3 * width)
    )
    grad_rows_part, gain_one_part, shift_one_part = first_pull(grad_normed)
    tokens_grad = (grad_middle + grad_rows_part).astype(jnp.bfloat16)
    layer_sums = (
        lax.psum_scatter(gain_one_part, ("dp", "head"), scatter_dimension=0, tiled=True),
        lax.psum_scatter(shift_one_part, ("dp", "head"), scatter_dimension=0, tiled=True),
        lax.psum_scatter(out_weight_part, ("dp", "head"), scatter_dimension=0, tiled=True),
        lax.psum_scatter(out_bias_part, ("dp", "head"), scatter_dimension=0, tiled=True),
        lax.psum_scatter(gain_two_part, ("dp", "head"), scatter_dimension=0, tiled=True),
        lax.psum_scatter(shift_two_part, ("dp", "head"), scatter_dimension=0, tiled=True),
        lax.psum_scatter(down_bias_part, ("dp", "head"), scatter_dimension=0, tiled=True),
    )
    head_sums = (
        lax.psum_scatter(qkv_weight_part, "dp", scatter_dimension=0, tiled=True),
        lax.psum_scatter(qkv_bias_part, "dp", scatter_dimension=1, tiled=True),
        lax.psum_scatter(up_weight_part, "dp", scatter_dimension=0, tiled=True),
        lax.psum_scatter(up_bias_part, "dp", scatter_dimension=0, tiled=True),
        lax.psum_scatter(down_weight_part, "dp", scatter_dimension=1, tiled=True),
    )
    return (
        layer_out,
        tokens_grad,
        layer_sums[0],
        layer_sums[1],
        head_sums[0],
        head_sums[1],
        layer_sums[2],
        layer_sums[3],
        layer_sums[4],
        layer_sums[5],
        head_sums[2],
        head_sums[3],
        head_sums[4],
        layer_sums[6],
    )


def solution(mesh):
    return jax.shard_map(
        local,
        mesh=mesh,
        in_specs=(
            P(("dp", "head"), None),
            P("dp"),
            P(("dp", "head")),
            P(("dp", "head")),
            P("dp", None, "head"),
            P(None, ("head", "dp")),
            P(("dp", "head"), None),
            P(("dp", "head")),
            P(("dp", "head")),
            P(("dp", "head")),
            P("dp", "head"),
            P(("head", "dp")),
            P("head", "dp"),
            P(("dp", "head")),
            P(("dp", "head"), None),
        ),
        out_specs=(
            P(("dp", "head"), None),
            P(("dp", "head"), None),
            P(("dp", "head")),
            P(("dp", "head")),
            P("dp", None, "head"),
            P(None, ("head", "dp")),
            P(("dp", "head"), None),
            P(("dp", "head")),
            P(("dp", "head")),
            P(("dp", "head")),
            P("dp", "head"),
            P(("head", "dp")),
            P("head", "dp"),
            P(("dp", "head")),
        ),
        check_vma=False,
    )
```

profile of v0, /device:TPU:0, one launch (start us, length us, event | category | flops | bytes accessed | tf_op | source)
XLA Modules:
  0.0 709.9 jit_solution(16283716665516034311)
XLA Ops:
  12.3 42.2 %all-reduce.21 = (bf16[768]{0:T(1024)(128)(2,1)S(1)}, bf16[768]{0:T(1024)(128)(2,1)S(1)}, bf16[768]{0:T(1024)(128)(2,1)S(1)}, bf16[768]{0:T(1024)(128)(2,1)S(1)}...) all-reduce(bf16[768]{0:T(1024)(128)(2,1)S(1)} %dynamic-update-slice, ...), channel_id=1, replica_groups=mesh['dp'=8,'head'=4] {'dp','head'}, use_global_device_ids=true, to_apply=%add.1 | all-reduce | flops 4608 | bytes 18432
  60.7 20.2 %all-gather.1 = bf16[8,24,2]{1,2,0:T(2,128)(2,1)S(1)} all-gather(bf16[1,24,2]{1,2,0:T(2,128)(2,1)S(1)} %bitcast.140), channel_id=1, replica_groups=mesh['dp'=8,'head'=4] {'dp'}, dimensions={0}, use_global_device_ids=true | all-gather | bytes 864 | tf_op jit(solution)/shard_map/all_gather | solution.py:63
  81.2 36.1 %all_gather.55 = bf16[768,3,192]{2,1,0:T(4,128)(2,1)S(1)} all-gather(bf16[96,3,192]{2,1,0:T(4,128)(2,1)S(1)} %copy.56), channel_id=1, replica_groups=mesh['dp'=8,'head'=4] {'dp'}, dimensions={0}, use_global_device_ids=true | all-gather | bytes 995328 | tf_op jit(solution)/shard_map/all_gather | solution.py:62
  125.0 5.0 reshape.198
  141.2 8.8 %all-to-all-done = bf16[4,370,192]{1,2,0:T(8,128)(2,1)S(1)} async-done(((bf16[4,370,192]{1,2,0:T(8,128)(2,1)}), bf16[4,370,192]{1,2,0:T(8,128)(2,1)S(1)}, u32[]{:S(2)}, u32[]{:S(2)}) %all-to-all-start) | async-done | bytes 568352 | tf_op jit(solution)/shard_map/all_to_all | solution.py:116
  157.2 20.8 %all-reduce.5 = bf16[768]{0:T(1024)(128)(2,1)S(1)} all-reduce(bf16[768]{0:T(1024)(128)(2,1)S(1)} %dynamic-update-slice.5), channel_id=1, replica_groups=mesh['dp'=8,'head'=4] {'dp'}, use_global_device_ids=true, to_apply=%add.5 | all-reduce | flops 768 | bytes 3072
  181.6 9.8 %all-gather.22.cloned.1.call-done = bf16[4,370,768]{2,1,0:T(8,128)(2,1)} async-done(((bf16[1,370,768]{2,1,0:T(8,128)(2,1)}), bf16[4,370,768]{2,1,0:T(8,128)(2,1)}) %all-gather.22.cloned.1.call-update) | async-done | bytes 2273296 | tf_op jit(solution)/shard_map/all_gather | solution.py:124
  195.0 39.5 %all-gather.14.cloned.1.call-done = bf16[768,768]{1,0:T(8,128)(2,1)} async-done(((bf16[96,768]{1,0:T(8,128)(2,1)}), bf16[768,768]{1,0:T(8,128)(2,1)}) %all-gather.14.cloned.1.call-update) | async-done | bytes 1179664 | tf_op jit(solution)/shard_map/all_gather | solution.py:64
  234.5 6.1 fusion.55
  240.6 35.8 %all-gather.16.cloned.1.call-done = bf16[768,768]{0,1:T(8,128)(2,1)} async-done(((bf16[768,96]{0,1:T(8,128)(2,1)}), bf16[768,768]{0,1:T(8,128)(2,1)}) %all-gather.16.cloned.1.call-update) | async-done | bytes 1179664 | tf_op jit(solution)/shard_map/all_gather | solution.py:66
  276.4 14.9 %convert_reduce_fusion = (f32[768]{0:T(1024)}, bf16[1480,768]{1,0:T(8,128)(2,1)S(1)}, f32[1480,768]{1,0:T(8,128)S(1)}) fusion(f32[1480,768]{1,0:T(8,128)} %fusion.55, f32[768]{0:T(1024)S(1)} %convert_element_type.133, bf16[1480,768]{1,0:T(8,128)(2,1)} %reshape.225, bf16[768,768]{0,1:T(8,128)(2,1)} %all-gather.16.cloned.1.call-done), kind=kOutput, calls=%fused_computation.8 | convolution fusion | flops 1831126272 | bytes 14825472 | tf_op jit(solution)/shard_map/dot_general | solution.py:25
  300.3 54.1 %fusion.46 = (bf16[376,768]{1,0:T(8,128)(2,1)S(1)}, bf16[376,768]{1,0:T(8,128)(2,1)S(1)}) fusion(bf16[1480,768]{1,0:T(8,128)(2,1)} %convolution_convert_fusion.1, bf16[1480,768]{1,0:T(8,128)(2,1)} %convolution_convert_fusion), kind=kCustom, calls=%all-reduce-scatter.2 | all-reduce-scatter fusion | flops 2310145 | bytes 5702144
  381.1 5.9 all-to-all-done.1
  408.5 5.7 fusion.56
  414.5 5.9 fusion.58
  420.4 5.9 fusion.59
  442.7 5.5 copy.75
  455.8 19.6 %all-reduce.20 = (f32[2,192]{1,0:T(2,128)S(1)}, f32[768]{0:T(1024)S(1)}) all-reduce(f32[2,192]{1,0:T(2,128)S(1)} %pad_maximum_fusion.2, f32[768]{0:T(1024)S(1)} %copy-done.28), channel_id=7, replica_groups=mesh['dp'=8,'head'=4] {'dp'}, use_global_device_ids=true, to_apply=%region_20.21.clone | all-reduce | flops 1152 | bytes 9216
  476.6 12.6 %all-to-all-done.2 = bf16[1480,3,192]{2,1,0:T(4,128)(2,1)} async-done(((bf16[1480,3,192]{2,1,0:T(4,128)(2,1)}), bf16[1480,3,192]{2,1,0:T(4,128)(2,1)}, u32[]{:S(2)}, u32[]{:S(2)}) %all-to-all-start.2) | async-done | bytes 1704992 | tf_op jit(solution)/shard_map/all_to_all | solution.py:191
  489.2 5.5 copy.76
  501.1 39.7 %all-reduce.19 = (f32[768]{0:T(1024)S(1)}, f32[768]{0:T(1024)S(1)}, f32[768]{0:T(1024)S(1)}, f32[768]{0:T(1024)S(1)}, f32[768]{0:T(1024)S(1)}, /*index=5*/f32[768]{0:T(1024)S(1)}) all-reduce(f32[768]{0:T(1024)S(1)} %get-tuple-element.18, f32[768]{0:T(1024)S(1)} %get-tuple-element.20, ...), channel_id=4, replica_groups=mesh['dp'=8,'head'=4] {'dp','head'}, use_global_device_ids=true, to_apply=%region_14.15.clone | all-reduce | flops 4608 | bytes 36864
  544.3 12.9 %reduce-scatter.10.cloned.1.call-done = f32[96,3,192]{2,0,1:T(8,128)} async-done(((f32[768,3,192]{2,0,1:T(8,128)}), f32[96,3,192]{2,0,1:T(8,128)}) %reduce-scatter.10.cloned.1.call-update) | async-done | bytes 221200 | tf_op jit(solution)/shard_map/reduce_scatter | solution.py:214
  557.2 72.8 %reduce-scatter.14.cloned.1.call-done = f32[96,768]{1,0:T(8,128)} async-done(((f32[768,768]{1,0:T(8,128)}), f32[96,768]{1,0:T(8,128)}) %reduce-scatter.14.cloned.1.call-update) | async-done | bytes 294928 | tf_op jit(solution)/shard_map/reduce_scatter | solution.py:216
  630.0 73.0 %reduce-scatter.16.cloned.1.call-done = f32[768,96]{0,1:T(8,128)} async-done(((f32[768,768]{0,1:T(8,128)}), f32[768,96]{0,1:T(8,128)}) %reduce-scatter.16.cloned.1.call-update) | async-done | bytes 294928 | tf_op jit(solution)/shard_map/reduce_scatter | solution.py:218
  (214 shorter events, 134.2 us)
Async XLA Ops:
  7.2 53.5 %copy-start.30 = (bf16[2,24]{1,0:T(2,128)(2,1)S(1)}, bf16[2,24]{1,0:T(2,128)(2,1)}, u32[]{:S(2)}) copy-start(bf16[2,24]{1,0:T(2,128)(2,1)} %param.20) | copy-start | bytes 292
  7.2 73.8 %copy-start.22 = (bf16[96,3,192]{2,0,1:T(8,128)(2,1)S(1)}, bf16[96,3,192]{2,0,1:T(8,128)(2,1)}, u32[]{:S(2)}) copy-start(bf16[96,3,192]{2,0,1:T(8,128)(2,1)} %param.19) | copy-start | bytes 331780
  7.2 111.2 %all-gather.20.cloned.1.call-start = ((), (), s32[]{:S(2)}) async-start(), calls=%async_computation.15 | async-start | bytes 2887680 | tf_op jit(solution)/shard_map/all_gather | solution.py:76
  57.0 61.1 %copy-start.23 = (f32[370]{0:T(512)}, f32[370]{0:T(512)S(1)}, u32[]{:S(2)}) copy-start(f32[370]{0:T(512)S(1)} %fusion.31) | copy-start | bytes 4444
  59.2 82.0 %all-gather.12.cloned.1.call-start = ((), (), s32[]{:S(2)}) async-start(), calls=%async_computation.7 | async-start | bytes 1216512 | tf_op jit(solution)/shard_map/all_gather | solution.py:55
  60.0 118.0 %all-gather.24.cloned.1.call-start = ((), (), s32[]{:S(2)}) async-start(), calls=%async_computation.17 | async-start | bytes 2887680 | tf_op jit(solution)/shard_map/all_gather | solution.py:145
  81.0 37.3 %copy-start.32 = (s32[8]{0:T(128)S(1)}, s32[8]{0:T(128)}, u32[]{:S(2)}) copy-start(s32[8]{0:T(128)} %param.16) | copy-start | bytes 100
  135.5 14.6 %copy-start.1 = (bf16[370,768]{1,0:T(8,128)(2,1)S(1)}, bf16[370,768]{1,0:T(8,128)(2,1)}, u32[]{:S(2)}) copy-start(bf16[370,768]{1,0:T(8,128)(2,1)} %param.15) | copy-start | bytes 1704964
  137.1 13.0 %all-to-all-start = ((bf16[4,370,192]{1,2,0:T(8,128)(2,1)}), bf16[4,370,192]{1,2,0:T(8,128)(2,1)S(1)}, u32[]{:S(2)}, u32[]{:S(2)}) async-start(bf16[4,370,192]{1,2,0:T(8,128)(2,1)} %copy.64), calls=%async_computation | async-start | bytes 1179648 | tf_op jit(solution)/shard_map/all_to_all | solution.py:116
  140.6 50.7 %all-gather.22.cloned.1.call-start = ((), (), s32[]{:S(2)}) async-start(), calls=%async_computation.16 | async-start | bytes 2887680 | tf_op jit(solution)/shard_map/all_gather | solution.py:124
  152.6 28.9 %copy-start.25 = (f32[370]{0:T(512)}, f32[370]{0:T(512)S(1)}, u32[]{:S(2)}) copy-start(f32[370]{0:T(512)S(1)} %multiply_reduce_fusion.1) | copy-start | bytes 4444
  153.7 80.8 %all-gather.14.cloned.1.call-start = ((), (), s32[]{:S(2)}) async-start(), calls=%async_computation.8 | async-start | bytes 1327104 | tf_op jit(solution)/shard_map/all_gather | solution.py:64
  154.3 122.1 %all-gather.16.cloned.1.call-start = ((), (), s32[]{:S(2)}) async-start(), calls=%async_computation.9 | async-start | bytes 1327104 | tf_op jit(solution)/shard_map/all_gather | solution.py:66
  154.9 339.8 %all-gather.18.cloned.1.call-start = ((), (), s32[]{:S(2)}) async-start(), calls=%async_computation.10 | async-start | bytes 4423680 | tf_op jit(solution)/shard_map/all_gather | solution.py:198
  276.4 14.9 %copy-start.10 = (f32[1480,768]{1,0:T(8,128)S(1)}, f32[1480,768]{1,0:T(8,128)}, u32[]{:S(2)}) copy-start(f32[1480,768]{1,0:T(8,128)} %fusion.55) | copy-start | bytes 13639684
  300.3 58.7 %copy-start.31 = (u32[32]{0:T(128)S(1)}, u32[32]{0:T(128)}, u32[]{:S(2)}) copy-start(u32[32]{0:T(128)} %constant.130) | copy-start | bytes 388
  354.4 6.4 collective-permute-start
  355.7 9.3 %collective-permute-start.1 = (bf16[18,768]{1,0:T(8,128)(2,1)S(1)}, bf16[18,768]{1,0:T(8,128)(2,1)S(1)}, u32[]{:S(2)}, u32[]{:S(2)}) collective-permute-start(bf16[18,768]{1,0:T(8,128)(2,1)S(1)} %slice.36), channel_id=1, source_target_pairs={{0,1},{1,2},{2,3},{4,5},{5,6},{6,7},{8,9},{9,10},{10,11},{12,13},{... | collective-permute-start | bytes 82952
  374.0 13.0 %all-to-all-start.1 = ((bf16[370,4,192]{0,2,1:T(8,128)(2,1)}), bf16[370,4,192]{0,2,1:T(8,128)(2,1)S(1)}, u32[]{:S(2)}, u32[]{:S(2)}) async-start(bf16[370,4,192]{0,2,1:T(8,128)(2,1)} %bitcast.133), calls=%async_computation.1 | async-start | bytes 1179648 | tf_op jit(solution)/shard_map/all_to_all | solution.py:160
  377.5 166.8 %reduce-scatter.12.cloned.1.call-start = ((), (), s32[]{:S(2)}) async-start(), calls=%async_computation.12 | async-start | bytes 2433024 | tf_op jit(solution)/shard_map/reduce_scatter | solution.py:207
  381.0 176.2 %reduce-scatter.10.cloned.1.call-start = ((), (), s32[]{:S(2)}) async-start(), calls=%async_computation.11 | async-start | bytes 2654208 | tf_op jit(solution)/shard_map/reduce_scatter | solution.py:214
  414.2 215.8 %reduce-scatter.14.cloned.1.call-start = ((), (), s32[]{:S(2)}) async-start(), calls=%async_computation.13 | async-start | bytes 2654208 | tf_op jit(solution)/shard_map/reduce_scatter | solution.py:216
  420.4 282.6 %reduce-scatter.16.cloned.1.call-start = ((), (), s32[]{:S(2)}) async-start(), calls=%async_computation.14 | async-start | bytes 2654208 | tf_op jit(solution)/shard_map/reduce_scatter | solution.py:218
  448.2 41.0 %all-to-all-start.2 = ((bf16[1480,3,192]{2,1,0:T(4,128)(2,1)}), bf16[1480,3,192]{2,1,0:T(4,128)(2,1)}, u32[]{:S(2)}, u32[]{:S(2)}) async-start(bf16[1480,3,192]{2,1,0:T(4,128)(2,1)} %copy.75), calls=%async_computation.2 | async-start | bytes 6062080 | tf_op jit(solution)/shard_map/all_to_all | solution.py:191
  (31 other events, 89.5 us)
Sparse Core Ops, SparseCore 0:
  59.3 23.5 all-gather.19
  85.9 55.2 all-gather.11
  142.8 22.6 all-gather.23
  167.5 23.7 all-gather.21
  193.3 41.1 all-gather.13
  236.5 39.8 all-gather.15
  277.9 29.4 all-gather.17
  384.2 100.1 reduce-scatter.11
  488.5 68.6 reduce-scatter.9
  561.1 68.8 reduce-scatter.13
  634.1 68.8 reduce-scatter.15
where the time goes:
time: 720 us; the launch traced here: 710 us
  waiting for transfers between devices  275 us (38%)
  blocking collectives  233 us (32%)
  local copies, waits for them, and re-layouts  78.2 us (11%)
  matrix products  68.1 us (9%)
  other arithmetic  21.6 us (3%)
  between operations  17.6 us (2%)
  starting transfers between devices  17.2 us (2%)
    unnamed x5, blocking collectives  176 us
    reduce_scatter x1, waiting for transfers between devices, local(): lax.psum_scatter(down_weight_part, 'dp', scatter_dimension=1, tiled=True)  73 us
    reduce_scatter x1, waiting for transfers between devices, local(): lax.psum_scatter(up_weight_part, 'dp', scatter_dimension=0, tiled=True)  72.8 us
    all_gather x1, waiting for transfers between devices, local(): lax.all_gather(up_weight, 'dp', axis=0, tiled=True)  39.5 us
    all_gather x1, blocking collectives, local(): lax.all_gather(qkv_weight, 'dp', axis=0, tiled=True)  36.1 us
    all_gather x1, waiting for transfers between devices, local(): lax.all_gather(down_weight, 'dp', axis=1, tiled=True)  35.8 us
    unnamed x111, local copies, waits for them, and re-layouts  34 us
    dot_general x4, matrix products, times_transposed(): lax.dot_general(former, latter, (((1,), (1,)), ((), ())), preferred_eleme...  23.3 us
  transfers between devices with their start and end apart: 16, of which 10 were waited for; matrix products, arithmetic and copies ran while one was open for 29% of the time, Pallas kernels for 0%

commit v1 on v0

--- a/solution.py
+++ b/solution.py
@@ -6,6 +6,18 @@
 
 HEAD_DIM = 64
 TEXT = 40
+
+
+def gather_by_bits(x, axis, dim):
+    ways, here = (lax.axis_size(axis), lax.axis_index(axis))
+    grown, reach = (x, 1)
+    while reach < ways:
+        theirs = lax.ppermute(grown, axis, [(d, d ^ reach) for d in range(ways)])
+        mine_first = jnp.concatenate([grown, theirs], axis=dim)
+        theirs_first = jnp.concatenate([theirs, grown], axis=dim)
+        grown = jnp.where(here & reach == 0, mine_first, theirs_first)
+        reach = 2 * reach
+    return grown
 
 
 def norm_rows(values, gain, shift):
@@ -63,7 +75,7 @@
         lax.all_gather(qkv_bias, "dp", axis=1, tiled=True),
         lax.all_gather(up_weight, "dp", axis=0, tiled=True),
         lax.all_gather(up_bias, "dp", axis=0, tiled=True),
-        lax.all_gather(down_weight, "dp", axis=1, tiled=True),
+        gather_by_bits(down_weight, "dp", 1),
     )
     local_width = w_qkv.shape[2]
     heads_local = local_width // HEAD_DIM

time: 720 us -> 722 us (level)
    unnamed x111 -> x109, local copies, waits for them, and re-layouts: 34 us -> 33.9 us
  transfers between devices with their start and end apart: 16 -> 19, of which waited for: 10 -> 10; matrix products, arithmetic and copies ran while one was open for 29% -> 29% of each run, Pallas kernels for 0% -> 0%
where the time goes in v1:
time: 722 us; the launch traced here: 711 us
  waiting for transfers between devices  273 us (38%)
  blocking collectives  232 us (32%)
  local copies, waits for them, and re-layouts  78.2 us (11%)
  matrix products  71.1 us (10%)
  other arithmetic  22 us (3%)
  between operations  17.7 us (2%)
  starting transfers between devices  17.3 us (2%)
    unnamed x5, blocking collectives  176 us
    reduce_scatter x1, waiting for transfers between devices, local(): lax.psum_scatter(down_weight_part, 'dp', scatter_dimension=1, tiled=True)  73 us
    reduce_scatter x1, waiting for transfers between devices, local(): lax.psum_scatter(up_weight_part, 'dp', scatter_dimension=0, tiled=True)  72.7 us
    all_gather x1, waiting for transfers between devices, local(): lax.all_gather(up_weight, 'dp', axis=0, tiled=True)  39.9 us
    all_gather x1, blocking collectives, local(): lax.all_gather(qkv_weight, 'dp', axis=0, tiled=True)  36.1 us
    all_gather x1, waiting for transfers between devices, local(): lax.all_gather(down_weight, 'dp', axis=1, tiled=True)  35.8 us
    unnamed x109, local copies, waits for them, and re-layouts  33.9 us
    dot_general x4, matrix products, times_transposed(): lax.dot_general(former, latter, (((1,), (1,)), ((), ())), preferred_eleme...  23.3 us
  transfers between devices with their start and end apart: 19, of which 10 were waited for; matrix products, arithmetic and copies ran while one was open for 29% of the time, Pallas kernels for 0%

profile of v1, /device:TPU:0, one launch (start us, length us, event | category | flops | bytes accessed | tf_op | source)
XLA Modules:
  0.0 711.3 jit_solution(17973257282652449783)
XLA Ops:
  12.3 42.2 %all-reduce.21 = (bf16[768]{0:T(1024)(128)(2,1)S(1)}, bf16[768]{0:T(1024)(128)(2,1)S(1)}, bf16[768]{0:T(1024)(128)(2,1)S(1)}, bf16[768]{0:T(1024)(128)(2,1)S(1)}...) all-reduce(bf16[768]{0:T(1024)(128)(2,1)S(1)} %dynamic-update-slice, ...), channel_id=1, replica_groups=mesh['dp'=8,'head'=4] {'dp','head'}, use_global_device_ids=true, to_apply=%add.1 | all-reduce | flops 4608 | bytes 18432
  60.7 20.2 %all-gather.1 = bf16[8,24,2]{1,2,0:T(2,128)(2,1)S(1)} all-gather(bf16[1,24,2]{1,2,0:T(2,128)(2,1)S(1)} %bitcast.139), channel_id=1, replica_groups=mesh['dp'=8,'head'=4] {'dp'}, dimensions={0}, use_global_device_ids=true | all-gather | bytes 864 | tf_op jit(solution)/shard_map/all_gather | solution.py:75
  81.2 36.1 %all_gather.54 = bf16[768,3,192]{2,1,0:T(4,128)(2,1)S(1)} all-gather(bf16[96,3,192]{2,1,0:T(4,128)(2,1)S(1)} %copy.56), channel_id=1, replica_groups=mesh['dp'=8,'head'=4] {'dp'}, dimensions={0}, use_global_device_ids=true | all-gather | bytes 995328 | tf_op jit(solution)/shard_map/all_gather | solution.py:74
  126.7 5.0 reshape.198
  142.3 9.4 %all-to-all-done = bf16[4,370,192]{1,2,0:T(8,128)(2,1)S(1)} async-done(((bf16[4,370,192]{1,2,0:T(8,128)(2,1)}), bf16[4,370,192]{1,2,0:T(8,128)(2,1)S(1)}, u32[]{:S(2)}, u32[]{:S(2)}) %all-to-all-start) | async-done | bytes 568352 | tf_op jit(solution)/shard_map/all_to_all | solution.py:128
  156.9 5.0 collective-permute-done
  163.6 20.5 %all-reduce.5 = bf16[768]{0:T(1024)(128)(2,1)S(1)} all-reduce(bf16[768]{0:T(1024)(128)(2,1)S(1)} %dynamic-update-slice.5), channel_id=1, replica_groups=mesh['dp'=8,'head'=4] {'dp'}, use_global_device_ids=true, to_apply=%add.5 | all-reduce | flops 768 | bytes 3072
  194.9 39.9 %all-gather.14.cloned.1.call-done = bf16[768,768]{1,0:T(8,128)(2,1)} async-done(((bf16[96,768]{1,0:T(8,128)(2,1)}), bf16[768,768]{1,0:T(8,128)(2,1)}) %all-gather.14.cloned.1.call-update) | async-done | bytes 1179664 | tf_op jit(solution)/shard_map/all_gather | solution.py:76
  234.8 6.1 fusion.62
  240.9 35.8 %all-gather.16.cloned.1.call-done = bf16[768,768]{0,1:T(8,128)(2,1)} async-done(((bf16[768,96]{0,1:T(8,128)(2,1)}), bf16[768,768]{0,1:T(8,128)(2,1)}) %all-gather.16.cloned.1.call-update) | async-done | bytes 1179664 | tf_op jit(solution)/shard_map/all_gather | solution.py:151
  276.7 14.9 %convert_reduce_fusion = (f32[768]{0:T(1024)}, bf16[1480,768]{1,0:T(8,128)(2,1)S(1)}, f32[1480,768]{1,0:T(8,128)S(1)}) fusion(f32[1480,768]{1,0:T(8,128)} %fusion.62, f32[768]{0:T(1024)S(1)} %convert_element_type.133, bf16[1480,768]{1,0:T(8,128)(2,1)} %reshape.225, bf16[768,768]{0,1:T(8,128)(2,1)} %all-gather.16.cloned.1.call-done), kind=kOutput, calls=%fused_computation.8 | convolution fusion | flops 1831126272 | bytes 14825472 | tf_op jit(solution)/shard_map/dot_general | solution.py:37
  301.9 54.1 %fusion.53 = (bf16[376,768]{1,0:T(8,128)(2,1)S(1)}, bf16[376,768]{1,0:T(8,128)(2,1)S(1)}) fusion(bf16[1480,768]{1,0:T(8,128)(2,1)} %convolution_convert_fusion.1, bf16[1480,768]{1,0:T(8,128)(2,1)} %convolution_convert_fusion), kind=kCustom, calls=%all-reduce-scatter.2 | all-reduce-scatter fusion | flops 2310145 | bytes 5702144
  382.7 5.9 all-to-all-done.1
  410.4 5.6 fusion.63
  416.3 5.9 fusion.65
  422.3 5.9 fusion.66
  444.5 5.5 copy.75
  457.6 19.7 %all-reduce.20 = (f32[2,192]{1,0:T(2,128)S(1)}, f32[768]{0:T(1024)S(1)}) all-reduce(f32[2,192]{1,0:T(2,128)S(1)} %pad_maximum_fusion.2, f32[768]{0:T(1024)S(1)} %copy-done.28), channel_id=7, replica_groups=mesh['dp'=8,'head'=4] {'dp'}, use_global_device_ids=true, to_apply=%region_20.21.clone | all-reduce | flops 1152 | bytes 9216
  478.5 12.5 %all-to-all-done.2 = bf16[1480,3,192]{2,1,0:T(4,128)(2,1)} async-done(((bf16[1480,3,192]{2,1,0:T(4,128)(2,1)}), bf16[1480,3,192]{2,1,0:T(4,128)(2,1)}, u32[]{:S(2)}, u32[]{:S(2)}) %all-to-all-start.2) | async-done | bytes 1704992 | tf_op jit(solution)/shard_map/all_to_all | solution.py:203
  491.0 5.6 copy.76
  503.0 39.5 %all-reduce.19 = (f32[768]{0:T(1024)S(1)}, f32[768]{0:T(1024)S(1)}, f32[768]{0:T(1024)S(1)}, f32[768]{0:T(1024)S(1)}, f32[768]{0:T(1024)S(1)}, /*index=5*/f32[768]{0:T(1024)S(1)}) all-reduce(f32[768]{0:T(1024)S(1)} %get-tuple-element.18, f32[768]{0:T(1024)S(1)} %get-tuple-element.20, ...), channel_id=4, replica_groups=mesh['dp'=8,'head'=4] {'dp','head'}, use_global_device_ids=true, to_apply=%region_14.15.clone | all-reduce | flops 4608 | bytes 36864
  545.9 12.7 %reduce-scatter.10.cloned.1.call-done = f32[96,3,192]{2,0,1:T(8,128)} async-done(((f32[768,3,192]{2,0,1:T(8,128)}), f32[96,3,192]{2,0,1:T(8,128)}) %reduce-scatter.10.cloned.1.call-update) | async-done | bytes 221200 | tf_op jit(solution)/shard_map/reduce_scatter | solution.py:226
  558.6 72.7 %reduce-scatter.14.cloned.1.call-done = f32[96,768]{1,0:T(8,128)} async-done(((f32[768,768]{1,0:T(8,128)}), f32[96,768]{1,0:T(8,128)}) %reduce-scatter.14.cloned.1.call-update) | async-done | bytes 294928 | tf_op jit(solution)/shard_map/reduce_scatter | solution.py:228
  631.4 73.0 %reduce-scatter.16.cloned.1.call-done = f32[768,96]{0,1:T(8,128)} async-done(((f32[768,768]{0,1:T(8,128)}), f32[768,96]{0,1:T(8,128)}) %reduce-scatter.16.cloned.1.call-update) | async-done | bytes 294928 | tf_op jit(solution)/shard_map/reduce_scatter | solution.py:230
  (220 shorter events, 140.0 us)
Async XLA Ops:
  7.2 53.6 %copy-start.30 = (bf16[2,24]{1,0:T(2,128)(2,1)S(1)}, bf16[2,24]{1,0:T(2,128)(2,1)}, u32[]{:S(2)}) copy-start(bf16[2,24]{1,0:T(2,128)(2,1)} %param.20) | copy-start | bytes 292
  7.2 73.8 %copy-start.22 = (bf16[96,3,192]{2,0,1:T(8,128)(2,1)S(1)}, bf16[96,3,192]{2,0,1:T(8,128)(2,1)}, u32[]{:S(2)}) copy-start(bf16[96,3,192]{2,0,1:T(8,128)(2,1)} %param.19) | copy-start | bytes 331780
  7.2 111.2 %all-gather.20.cloned.1.call-start = ((), (), s32[]{:S(2)}) async-start(), calls=%async_computation.15 | async-start | bytes 2887680 | tf_op jit(solution)/shard_map/all_gather | solution.py:88
  57.0 61.1 %copy-start.23 = (f32[370]{0:T(512)}, f32[370]{0:T(512)S(1)}, u32[]{:S(2)}) copy-start(f32[370]{0:T(512)S(1)} %fusion.37) | copy-start | bytes 4444
  59.2 83.1 %all-gather.12.cloned.1.call-start = ((), (), s32[]{:S(2)}) async-start(), calls=%async_computation.7 | async-start | bytes 1216512 | tf_op jit(solution)/shard_map/all_gather | solution.py:67
  60.0 124.5 %all-gather.24.cloned.1.call-start = ((), (), s32[]{:S(2)}) async-start(), calls=%async_computation.17 | async-start | bytes 2887680 | tf_op jit(solution)/shard_map/all_gather | solution.py:157
  81.0 37.3 %copy-start.32 = (s32[8]{0:T(128)S(1)}, s32[8]{0:T(128)}, u32[]{:S(2)}) copy-start(s32[8]{0:T(128)} %param.16) | copy-start | bytes 100
  138.7 13.0 %all-to-all-start = ((bf16[4,370,192]{1,2,0:T(8,128)(2,1)}), bf16[4,370,192]{1,2,0:T(8,128)(2,1)S(1)}, u32[]{:S(2)}, u32[]{:S(2)}) async-start(bf16[4,370,192]{1,2,0:T(8,128)(2,1)} %copy.64), calls=%async_computation | async-start | bytes 1179648 | tf_op jit(solution)/shard_map/all_to_all | solution.py:128
  142.2 49.1 %all-gather.22.cloned.1.call-start = ((), (), s32[]{:S(2)}) async-start(), calls=%async_computation.16 | async-start | bytes 2887680 | tf_op jit(solution)/shard_map/all_gather | solution.py:136
  155.4 79.4 %all-gather.14.cloned.1.call-start = ((), (), s32[]{:S(2)}) async-start(), calls=%async_computation.8 | async-start | bytes 1327104 | tf_op jit(solution)/shard_map/all_gather | solution.py:76
  156.0 120.7 %all-gather.16.cloned.1.call-start = ((), (), s32[]{:S(2)}) async-start(), calls=%async_computation.9 | async-start | bytes 1327104 | tf_op jit(solution)/shard_map/all_gather | solution.py:151
  156.6 340.0 %all-gather.18.cloned.1.call-start = ((), (), s32[]{:S(2)}) async-start(), calls=%async_computation.10 | async-start | bytes 4423680 | tf_op jit(solution)/shard_map/all_gather | solution.py:210
  156.6 5.3 collective-permute-start
  162.0 22.2 %collective-permute-start.1 = (bf16[768,192]{0,1:T(8,128)(2,1)S(1)}, bf16[768,192]{0,1:T(8,128)(2,1)S(1)}, u32[]{:S(2)}, u32[]{:S(2)}) collective-permute-start(bf16[768,192]{0,1:T(8,128)(2,1)S(1)} %maximum_select_fusion.3), channel_id=1, source_target_pairs={{0,8},{4,12},{8,0},{12,4},{16,24},{20,28},{24,16},{28,20},{1,9},{5... | collective-permute-start | bytes 884744 | tf_op jit(solution)/shard_map/ppermute | solution.py:15
  184.4 112.8 %collective-permute-start.2 = (bf16[768,384]{0,1:T(8,128)(2,1)S(1)}, bf16[768,384]{0,1:T(8,128)(2,1)}, u32[]{:S(2)}, u32[]{:S(2)}) collective-permute-start(bf16[768,384]{0,1:T(8,128)(2,1)S(1)} %maximum_select_fusion.2), channel_id=1, source_target_pairs={{0,16},{4,20},{8,24},{12,28},{16,0},{20,4},{24,8},{28,12},{1,17},{... | collective-permute-start | bytes 1769480 | tf_op jit(solution)/shard_map/ppermute | solution.py:15
  301.9 58.7 %copy-start.31 = (u32[32]{0:T(128)S(1)}, u32[32]{0:T(128)}, u32[]{:S(2)}) copy-start(u32[32]{0:T(128)} %constant.144) | copy-start | bytes 388
  356.0 6.4 collective-permute-start.3
  357.4 9.3 %collective-permute-start.4 = (bf16[18,768]{1,0:T(8,128)(2,1)S(1)}, bf16[18,768]{1,0:T(8,128)(2,1)S(1)}, u32[]{:S(2)}, u32[]{:S(2)}) collective-permute-start(bf16[18,768]{1,0:T(8,128)(2,1)S(1)} %slice.36), channel_id=1, source_target_pairs={{0,1},{1,2},{2,3},{4,5},{5,6},{6,7},{8,9},{9,10},{10,11},{12,13},{... | collective-permute-start | bytes 82952
  375.6 13.0 %all-to-all-start.1 = ((bf16[370,4,192]{0,2,1:T(8,128)(2,1)}), bf16[370,4,192]{0,2,1:T(8,128)(2,1)S(1)}, u32[]{:S(2)}, u32[]{:S(2)}) async-start(bf16[370,4,192]{0,2,1:T(8,128)(2,1)} %bitcast.132), calls=%async_computation.1 | async-start | bytes 1179648 | tf_op jit(solution)/shard_map/all_to_all | solution.py:172
  379.1 166.8 %reduce-scatter.12.cloned.1.call-start = ((), (), s32[]{:S(2)}) async-start(), calls=%async_computation.12 | async-start | bytes 2433024 | tf_op jit(solution)/shard_map/reduce_scatter | solution.py:219
  382.7 176.0 %reduce-scatter.10.cloned.1.call-start = ((), (), s32[]{:S(2)}) async-start(), calls=%async_computation.11 | async-start | bytes 2654208 | tf_op jit(solution)/shard_map/reduce_scatter | solution.py:226
  416.1 215.3 %reduce-scatter.14.cloned.1.call-start = ((), (), s32[]{:S(2)}) async-start(), calls=%async_computation.13 | async-start | bytes 2654208 | tf_op jit(solution)/shard_map/reduce_scatter | solution.py:228
  422.2 282.1 %reduce-scatter.16.cloned.1.call-start = ((), (), s32[]{:S(2)}) async-start(), calls=%async_computation.14 | async-start | bytes 2654208 | tf_op jit(solution)/shard_map/reduce_scatter | solution.py:230
  450.0 41.0 %all-to-all-start.2 = ((bf16[1480,3,192]{2,1,0:T(4,128)(2,1)}), bf16[1480,3,192]{2,1,0:T(4,128)(2,1)}, u32[]{:S(2)}, u32[]{:S(2)}) async-start(bf16[1480,3,192]{2,1,0:T(4,128)(2,1)} %copy.75), calls=%async_computation.2 | async-start | bytes 6062080 | tf_op jit(solution)/shard_map/all_to_all | solution.py:203
  (33 other events, 154.7 us)
Sparse Core Ops, SparseCore 0:
  59.4 23.5 all-gather.19
  85.9 55.2 all-gather.11
  142.8 22.7 all-gather.23
  167.6 23.6 all-gather.21
  193.3 41.4 all-gather.13
  236.8 39.8 all-gather.15
  278.2 29.4 all-gather.17
  385.8 100.0 reduce-scatter.11
  489.9 68.6 reduce-scatter.9
  562.5 68.7 reduce-scatter.13
  635.4 68.8 reduce-scatter.15
